TPU v7x, 32 devices: a whole 2x2x4 slice. The times are simulated.
32 devices in a mesh: hap: 16 (over z, x, core), mk: 2 (over y).
Axes of the slice: x: 2, y: 2, z: 4, core: 2. Of those that a mesh axis runs over, the one named last changes fastest.
Arguments:
- posterior: bfloat16 [10, 1024, 16384], P('mk', None, 'hap'), may hold values from 0 to 1, as said below
- alleles: int32 [16384, 64], P('hap', 'mk'), may hold values from 0 to 1
- owner_map: int32 [1024], replicated, may hold values from 0 to 31, as said below
Outputs:
- dosage: float32 [1024, 64], P(('hap', 'mk'))
Inputs may be any that keep to these rules, and one draw needn't show every extreme that they name: `owner_map`: every device index is named by exactly 32 targets. `posterior`: every entry is positive.
All inputs are finite; a program needn't handle non-finite values.
Results may differ from a plain program's by a relative error of at most 0.0003.
Values sent between devices are 32-bit elements; how exact they have to be, the bound alone decides.
A program may use at most 64 MiB of HBM per device.

v0:
```python
import jax
import jax.numpy as jnp
from jax import lax
from jax.sharding import PartitionSpec as P


def interpolate_used(column_sums, denominator):
    intervals = denominator.shape[0] - 1
    targets = denominator.shape[1]
    marker_span = column_sums.shape[2]
    weight = (jnp.arange(marker_span, dtype=jnp.float32) + 0.5) / marker_span
    left_ratio = column_sums[:intervals] / denominator[:-1, :, None]
    right_ratio = column_sums[intervals:] / denominator[1:, :, None]
    blended = (1.0 - weight) * left_ratio + weight * right_ratio
    return jnp.transpose(blended, (1, 0, 2)).reshape(targets, intervals * marker_span)


def positions(owner_map, devices, per_device):
    owner_table = (owner_map[:, None] == jnp.arange(devices, dtype=jnp.int32)[None, :]).astype(
        jnp.int32
    )
    owner_rank = jnp.sum(jnp.cumsum(owner_table, axis=0) * owner_table, axis=1) - 1
    return owner_map * per_device + owner_rank


def select_rows(row_of, first_row, count, source):
    wanted_rows = first_row + jnp.arange(count, dtype=jnp.int32)
    selector = (row_of[None, :] == wanted_rows[:, None]).astype(jnp.float32)
    return jnp.dot(
        selector, source, precision=lax.Precision.HIGHEST, preferred_element_type=jnp.float32
    )


def on_device(posterior, alleles, owner_map):
    targets = posterior.shape[1]
    anchors = posterior.shape[0]
    allele_bf = alleles.astype(jnp.bfloat16)
    unit_vector = jnp.ones((posterior.shape[2],), jnp.bfloat16)
    denominator = jnp.einsum(
        "kth,h->kt", posterior, unit_vector, preferred_element_type=jnp.float32
    )
    marker_span = alleles.shape[1] // (anchors - 1)
    padded = jnp.pad(allele_bf, ((0, 0), (marker_span, marker_span)))
    window = jnp.stack(
        [padded[:, anchor * marker_span : (anchor + 2) * marker_span] for anchor in range(anchors)]
    )
    products = jnp.einsum("kth,khs->kts", posterior, window, preferred_element_type=jnp.float32)
    column_sums = jnp.concatenate(
        [products[:-1, :, marker_span:], products[1:, :, :marker_span]], axis=0
    )
    hap_count = lax.axis_size("hap")
    mk_count = lax.axis_size("mk")
    devices = hap_count * mk_count
    per_device = targets // devices
    row_of = positions(owner_map, devices, per_device)
    totals = lax.psum((column_sums, denominator), "hap")
    block_dose = interpolate_used(totals[0], totals[1])
    all_markers = lax.all_gather(block_dose, "mk", axis=1, tiled=True)
    device_id = lax.axis_index("hap") * mk_count + lax.axis_index("mk")
    return select_rows(row_of, device_id * per_device, per_device, all_markers)


def solution(mesh):
    placed = (P("mk", None, "hap"), P("hap", "mk"), P())
    return jax.shard_map(
        on_device, mesh=mesh, in_specs=placed, out_specs=P(("hap", "mk"), None), check_vma=False
    )
```

profile of v0, /device:TPU:0, one launch (start us, length us, event | category | flops | bytes accessed | tf_op | source)
XLA Modules:
  0.0 123.1 jit_solution(12400654508834789162)
XLA Ops:
  6.5 0.0 all-reduce.3.cloned.1.call-start
  6.5 0.9 convert_element_type.12
  7.5 0.0 copy-start
  7.5 6.8 %convolution_bitcast_fusion = f32[5,1024,16]{1,2,0:T(8,128)S(1)} fusion(bf16[5,1024,16]{1,2,0:T(8,128)(2,1)S(1)} %fusion.14, bf16[5,1024,1024]{2,1,0:T(8,128)(2,1)} %param.3), kind=kOutput, calls=%fused_computation | convolution fusion | flops 167772160 | bytes 10977280 | tf_op jit(solution)/shard_map/kth,khs->kts/dot_general | solution.py:47
  14.4 0.7 pad_maximum_fusion
  15.1 0.0 all-reduce.3.cloned.1.call-update
  15.1 6.8 %fusion.18 = f32[1,5,1024]{2,0,1:T(1,128)S(1)} fusion(bf16[5,1024,1024]{2,1,0:T(8,128)(2,1)} %param.3), kind=kOutput, calls=%fused_computation.33 | convolution fusion | flops 10485760 | bytes 10506240 | tf_op jit(solution)/shard_map/kth,h->kt/dot_general | solution.py:39
  21.9 63.0 %psum.15 = f32[5,1024]{1,0:T(8,128)S(1)} all-reduce(f32[5,1024]{1,0:T(8,128)S(1)} %bitcast.49), channel_id=1, replica_groups=mesh['hap'=16,'mk'=2] {'hap'}, use_global_device_ids=true, to_apply=%region_4.5 | all-reduce | flops 5120 | bytes 40960 | tf_op jit(solution)/shard_map/psum | solution.py:56
  84.9 0.0 copy-done
  85.0 9.0 %reduce-window.6 = s32[32,8,128]{2,1,0:T(8,128)S(1)} reduce-window(s32[32,8,128]{2,1,0:T(8,128)S(1)} %fusion.6, s32[]{:T(128)} %constant.12.clone.1), window={size=1x1x128 pad=0_0x0_0x127_0}, to_apply=%region_0.1 | reduce-window | flops 4161536 | bytes 262148 | tf_op jit(solution)/shard_map/reduce-window
  94.0 0.1 slice.55
  94.1 0.1 copy.4
  94.3 0.1 copy.5
  94.3 0.1 broadcast_add_fusion
  94.5 13.3 %all-reduce.3.cloned.1.call-done = f32[8,1024,8]{1,2,0:T(8,128)} async-done(((f32[8,1024,8]{1,2,0:T(8,128)}), f32[8,1024,8]{1,2,0:T(8,128)}) %all-reduce.3.cloned.1.call-update) | async-done | bytes 262160 | tf_op jit(solution)/shard_map/psum | solution.py:56
  107.8 1.1 fusion.4
  108.9 6.5 %all_gather.3 = f32[1024,64]{0,1:T(8,128)S(1)} all-gather(f32[1024,32]{0,1:T(8,128)S(1)} %fusion.4), channel_id=1, replica_groups=mesh['hap'=16,'mk'=2] {'mk'}, dimensions={1}, use_global_device_ids=true | all-gather | bytes 393216 | tf_op jit(solution)/shard_map/all_gather | solution.py:58
  115.4 0.9 fusion.7
  (15 shorter events, 0.2 us)
Async XLA Ops:
  6.5 101.3 %all-reduce.3.cloned.1.call-start = ((), (), s32[]{:S(2)}) async-start(), calls=%async_computation | async-start | bytes 524288 | tf_op jit(solution)/shard_map/psum | solution.py:56
  7.5 77.4 %copy-start = (s32[1024]{0:T(1024)S(1)}, s32[1024]{0:T(1024)}, u32[]{:S(2)}) copy-start(s32[1024]{0:T(1024)} %param.5) | copy-start | bytes 12292
Sparse Core Ops, SparseCore 0:
  15.2 92.5 all-reduce.2
where the time goes:
time: 123 us
  blocking collectives  69.5 us (57%)
  matrix products  14.5 us (12%)
  between operations  13.5 us (11%)
  waiting for transfers between devices  13.3 us (11%)
  other arithmetic  11.9 us (10%)
    psum x1, blocking collectives, on_device(): totals = lax.psum((column_sums, denominator), 'hap')  63 us
    psum x1, waiting for transfers between devices, on_device(): totals = lax.psum((column_sums, denominator), 'hap')  13.3 us
    another operation x3, other arithmetic  9.15 us
    dot_general x1, matrix products, on_device(): jnp.einsum('kth,khs->kts', posterior, window, preferred_element_type=jnp....  6.8 us
    dot_general x1, matrix products, on_device(): jnp.einsum('kth,h->kt', posterior, unit_vector, preferred_element_type=jn...  6.78 us
    all_gather x1, blocking collectives, on_device(): all_markers = lax.all_gather(block_dose, 'mk', axis=1, tiled=True)  6.51 us
  transfers between devices with their start and end apart: 1, of which 1 were waited for; matrix products, arithmetic and copies ran while one was open for 13% of the time, Pallas kernels for 0%

commit v1 on v0

v1 whole, which is shorter than its diff:
```python
import functools

import jax
import jax.numpy as jnp
from jax import lax
from jax.experimental import pallas as pl
from jax.experimental.pallas import tpu as pltpu
from jax.sharding import PartitionSpec as P

LANES = 128
HALF = LANES // 2
CORES = 2
MESH = pl.DeviceIdType.MESH
F32 = jnp.float32
BF16 = jnp.bfloat16


def own_rows(ref, index, count):
    if count % 8 == 0:
        return ref[pl.ds(pl.multiple_of(index * count, 8), count), :]
    pieces = 8 // count
    tile = ref[pl.ds(pl.multiple_of((index // pieces) * 8, 8), 8), :]
    rows = tile[:count]
    for piece in range(1, pieces):
        rows = jnp.where(index % pieces == piece, tile[piece * count : (piece + 1) * count], rows)
    return rows


def kernel(
    hap_count,
    mk_count,
    steps,
    post_hbm,
    allele_hbm,
    owner_hbm,
    out_ref,
    post,
    allele,
    owner,
    weights,
    choose,
    parts,
    mine,
    pair_in,
    reduced,
    chip_in,
    final,
    turned,
    post_sem,
    small_sem,
    pair_send,
    pair_recv,
    chip_send,
    chip_recv,
    final_send,
    final_recv,
):
    anchors, targets, _ = post.shape
    block = allele.shape[0]
    intervals = anchors - 1
    span = block // intervals
    local = intervals // CORES
    body = 2 * local * span
    rows_kept = mine.shape[1] // CORES
    chips = hap_count // CORES
    per_chip = targets // chips
    devices = hap_count * mk_count
    per_device = targets // devices
    group = CORES * mk_count
    chunk = targets // steps

    hap, mk = lax.axis_index("hap"), lax.axis_index("mk")
    chip, core = hap // CORES, hap % CORES
    place = mk * CORES + core

    def chip_peer(step):
        return {"hap": ((chip + step) % chips) * CORES + core, "mk": mk}

    def group_peer(step):
        other = (place + step) % group
        return {"hap": chip * CORES + other % CORES, "mk": other // CORES}

    allele_copy = pltpu.make_async_copy(allele_hbm, allele, small_sem.at[0])
    owner_copy = pltpu.make_async_copy(owner_hbm, owner, small_sem.at[1])
    owner_copy.start()
    allele_copy.start()
    post_copies = []
    for i in range(steps):
        rows = pl.ds(i * chunk, chunk)
        copy = pltpu.make_async_copy(post_hbm.at[:, rows, :], post.at[:, rows, :], post_sem.at[i])
        copy.start()
        post_copies.append(copy)

    barrier = pltpu.get_barrier_semaphore()
    for step in range(1, chips):
        pl.semaphore_signal(barrier, inc=1, device_id=chip_peer(step), device_id_type=MESH)
    for step in range(1, group):
        pl.semaphore_signal(barrier, inc=1, device_id=group_peer(step), device_id_type=MESH)

    owner_copy.wait()
    owners = owner[...]
    table = (lax.broadcasted_iota(jnp.int32, (devices, targets), 0) == owners).astype(F32)
    before = (
        lax.broadcasted_iota(jnp.int32, (LANES, LANES), 0)
        < lax.broadcasted_iota(jnp.int32, (LANES, LANES), 1)
    ).astype(F32).astype(BF16)
    carry = jnp.zeros((devices, 1), F32)
    ranks = []
    for b in range(targets // LANES):
        piece = table[:, b * LANES : (b + 1) * LANES]
        count = jnp.dot(piece.astype(BF16), before, preferred_element_type=F32) + carry
        ranks.append(jnp.sum(piece * count, axis=0, keepdims=True))
        carry = carry + jnp.sum(piece, axis=1, keepdims=True)
    row_of = owners.astype(F32) * per_device + jnp.concatenate(ranks, axis=1)

    order = sorted(range(1, chips), key=lambda s: abs(s - chips // 2 - 0.5)) + [0]

    for step in order:
        first = ((chip + step) % chips) * per_chip
        wanted = (lax.broadcasted_iota(jnp.int32, (per_chip, targets), 0) + first).astype(F32)
        choose[step] = (wanted == row_of).astype(F32).astype(BF16)

    allele_copy.wait()
    col = lax.broadcasted_iota(jnp.int32, (block, LANES), 1)
    marker = lax.broadcasted_iota(jnp.int32, (block, LANES), 0)
    lane = lax.broadcasted_iota(jnp.int32, (1, LANES), 1)
    spread = jnp.zeros((block, LANES), F32)
    starts = []
    for j in range(intervals):
        for side in range(2):
            start = (j // local) * HALF + (j % local) * 2 * span + side * span
            starts.append((j + side, start))
            hit = (col - start == marker - j * span) & (col >= start) & (col < start + span)
            spread = spread + hit.astype(F32)
    wide = lax.dot_general(
        allele[...].astype(F32).astype(BF16),
        spread.astype(BF16),
        (((0,), (0,)), ((), ())),
        preferred_element_type=F32,
    )
    for k in range(anchors):
        inside = jnp.zeros((1, LANES), F32)
        for anchor, start in starts:
            if anchor == k:
                inside = inside + ((lane >= start) & (lane < start + span)).astype(F32)
        ones = jnp.zeros((1, LANES), F32)
        for c in range(CORES):
            if c * local <= k <= (c + 1) * local:
                ones = ones + (lane == c * HALF + body + k - c * local).astype(F32)
        weights[k] = (wide * inside + ones).astype(BF16)

    for i in range(steps):
        rows = pl.ds(i * chunk, chunk)
        post_copies[i].wait()
        total = jnp.dot(post[0, rows, :], weights[0], preferred_element_type=F32)
        for k in range(1, anchors):
            total = total + jnp.dot(post[k, rows, :], weights[k], preferred_element_type=F32)
        high = total.astype(BF16)
        parts[rows, pl.ds(0, LANES)] = high
        parts[rows, pl.ds(LANES, LANES)] = (total - high.astype(F32)).astype(BF16)

    pl.semaphore_wait(barrier, chips - 1 + group - 1)

    kept = pl.ds(pl.multiple_of(core * rows_kept, 8), rows_kept)
    given = pl.ds(pl.multiple_of((1 - core) * rows_kept, 8), rows_kept)
    pair_copies = {}
    for step in order:
        both = jnp.dot(choose[step], parts[...], preferred_element_type=F32)
        sums = jnp.transpose(both[:, :LANES] + both[:, LANES:])
        for c in range(CORES):
            mine[step, pl.ds(c * rows_kept, rows_kept), :] = sums[c * HALF : c * HALF + rows_kept]
        copy = pltpu.make_async_remote_copy(
            src_ref=mine.at[step, given],
            dst_ref=pair_in.at[step],
            send_sem=pair_send.at[step],
            recv_sem=pair_recv.at[step],
            device_id={"hap": chip * CORES + 1 - core, "mk": mk},
            device_id_type=MESH,
        )
        copy.start()
        pair_copies[step] = copy

    chip_copies = {}
    for step in order:
        pair_copies[step].wait_recv()
        reduced[step] = mine[step, kept, :] + pair_in[step]
        if step:
            copy = pltpu.make_async_remote_copy(
                src_ref=reduced.at[step],
                dst_ref=chip_in.at[step],
                send_sem=chip_send.at[step],
                recv_sem=chip_recv.at[step],
                device_id=chip_peer(step),
                device_id_type=MESH,
            )
            copy.start()
            chip_copies[step] = copy

    total = reduced[0]
    for step in reversed(order[:-1]):
        chip_copies[step].wait_recv()
        total = total + chip_in[step]

    weight = (lax.broadcasted_iota(jnp.int32, (span, per_chip), 0).astype(F32) + 0.5) / span
    for l in range(local):
        base = 2 * l * span
        left = total[base : base + span] / total[body + l : body + l + 1]
        right = total[base + span : base + 2 * span] / total[body + l + 1 : body + l + 2]
        final[place, pl.ds(l * span, span), :] = (1.0 - weight) * left + weight * right

    final_copies = {}
    for step in range(1, group):
        copy = pltpu.make_async_remote_copy(
            src_ref=final.at[place],
            dst_ref=final.at[place],
            send_sem=final_send.at[step],
            recv_sem=final_recv.at[step],
            device_id=group_peer(step),
            device_id_type=MESH,
        )
        copy.start()
        final_copies[step] = copy
    for step in range(1, group):
        source = (place + group - step) % group
        pltpu.make_async_remote_copy(
            src_ref=final.at[source],
            dst_ref=final.at[source],
            send_sem=final_send.at[step],
            recv_sem=final_recv.at[step],
            device_id=group_peer(step),
            device_id_type=MESH,
        ).wait_recv()

    all_markers = final[...].reshape(group * local * span, per_chip)
    turned[...] = jnp.transpose(all_markers)
    out_ref[...] = own_rows(turned, core * mk_count + mk, per_device)

    for step in order:
        pair_copies[step].wait_send()
        if step:
            chip_copies[step].wait_send()
    for step in range(1, group):
        final_copies[step].wait_send()


def solution(mesh):
    hap_count, mk_count = mesh.shape["hap"], mesh.shape["mk"]
    steps = 4

    def on_device(posterior, alleles, owner_map):
        anchors, targets, refs = posterior.shape
        block = alleles.shape[1]
        intervals = anchors - 1
        local = intervals // CORES
        span = block // intervals
        chips = hap_count // CORES
        per_chip = targets // chips
        per_device = targets // (hap_count * mk_count)
        group = CORES * mk_count
        rows_kept = -(-(2 * local * span + local + 1) // 8) * 8
        scratch = [
            pltpu.VMEM(posterior.shape, BF16),
            pltpu.VMEM((block, refs), jnp.int32),
            pltpu.VMEM((1, targets), jnp.int32),
            pltpu.VMEM((anchors, refs, LANES), BF16),
            pltpu.VMEM((chips, per_chip, targets), BF16),
            pltpu.VMEM((targets, 2 * LANES), BF16),
            pltpu.VMEM((chips, CORES * rows_kept, per_chip), F32),
            pltpu.VMEM((chips, rows_kept, per_chip), F32),
            pltpu.VMEM((chips, rows_kept, per_chip), F32),
            pltpu.VMEM((chips, rows_kept, per_chip), F32),
            pltpu.VMEM((group, local * span, per_chip), F32),
            pltpu.VMEM((per_chip, mk_count * block), F32),
            pltpu.SemaphoreType.DMA((steps,)),
            pltpu.SemaphoreType.DMA((2,)),
        ] + [pltpu.SemaphoreType.DMA((chips,))] * 4 + [pltpu.SemaphoreType.DMA((group,))] * 2
        return pl.pallas_call(
            functools.partial(kernel, hap_count, mk_count, steps),
            out_shape=jax.ShapeDtypeStruct((per_device, mk_count * block), F32),
            in_specs=[pl.BlockSpec(memory_space=pltpu.HBM)] * 3,
            out_specs=pl.BlockSpec(memory_space=pltpu.VMEM),
            scratch_shapes=scratch,
            compiler_params=pltpu.CompilerParams(
                collective_id=0, has_side_effects=True, vmem_limit_bytes=48 * 1024 * 1024
            ),
        )(posterior, alleles.T, owner_map.reshape(1, targets))

    placed = (P("mk", None, "hap"), P("hap", "mk"), P())
    return jax.shard_map(
        on_device, mesh=mesh, in_specs=placed, out_specs=P(("hap", "mk"), None), check_vma=False
    )
```

time: 123 us -> 23.5 us (0.19)
  blocking collectives: 69.5 us -> 0 us
  Pallas kernels: 0 us -> 21.1 us
  matrix products: 14.5 us -> 0 us
  between operations: 13.5 us -> 0.01 us
  waiting for transfers between devices: 13.3 us -> 0 us
  other arithmetic: 11.9 us -> 0 us
  local copies, waits for them, and re-layouts: 0.38 us -> 2.2 us
    psum x1 -> x0, blocking collectives: 63 us -> none  [on_device(): totals = lax.psum((column_sums, denominator), 'hap')]
    pallas_call x0 -> x1, Pallas kernels: none -> 21.1 us  [on_device(): pl.pallas_call(functools.partial(kernel, hap_count, mk_count, steps), out...]
    dot_general x3 -> x0, matrix products: 14.5 us -> none  [the longest x1 6.8 us: on_device(): jnp.einsum('kth,khs->kts', posterior, window, preferred_element_type=jnp....]
    psum x1 -> x0, waiting for transfers between devices: 13.3 us -> none  [on_device(): totals = lax.psum((column_sums, denominator), 'hap')]
    another operation x3 -> x0, other arithmetic: 9.15 us -> none
    all_gather x1 -> x0, blocking collectives: 6.51 us -> none  [on_device(): all_markers = lax.all_gather(block_dose, 'mk', axis=1, tiled=True)]
    unnamed x6 -> x5, local copies, waits for them, and re-layouts: 0.02 us -> 2.2 us
  transfers between devices with their start and end apart: 1 -> 0, of which waited for: 1 -> 0; matrix products, arithmetic and copies ran while one was open for 13% -> 0% of each run, Pallas kernels for 0% -> 0%
where the time goes in v1:
time: 23.5 us; the launch traced here: 23.3 us
  Pallas kernels  21.1 us (90%)
  local copies, waits for them, and re-layouts  2.2 us (9%)
    pallas_call x1, Pallas kernels, on_device(): pl.pallas_call(functools.partial(kernel, hap_count, mk_count, steps), out...  21.1 us
    unnamed x5, local copies, waits for them, and re-layouts  2.2 us

profile of v1, /device:TPU:0, one launch (start us, length us, event | category | flops | bytes accessed | tf_op | source)
XLA Modules:
  0.0 23.3 jit_solution(12672234304036369069)
XLA Ops:
  0.0 0.0 copy-start
  0.0 0.9 %copy-done = s32[1024,32]{0,1:T(8,128)S(1)} copy-done((s32[1024,32]{0,1:T(8,128)S(1)}, s32[1024,32]{0,1:T(8,128)}, u32[]{:S(2)}) %copy-start) | copy-done | bytes 131096
  0.9 0.0 copy-start.1
  0.9 0.7 %copy-done.1 = s32[1024]{0:T(1024)S(1)} copy-done((s32[1024]{0:T(1024)S(1)}, s32[1024]{0:T(1024)}, u32[]{:S(2)}) %copy-start.1) | copy-done | bytes 4120
  1.6 21.1 %shard_map.37 = f32[32,64]{1,0:T(8,128)S(1)} custom-call(bf16[5,1024,1024]{2,1,0:T(8,128)(2,1)} %post_hbm.1, s32[32,1024]{1,0:T(8,128)S(1)} %bitcast.2, s32[1,1024]{1,0:T(1,128)S(1)} %bitcast.3), custom_call_target="tpu_custom_call" | custom-call | tf_op jit(solution)/shard_map/pallas_call | solution.py:277
  22.7 0.6 %copy.5 = f32[32,64]{1,0:T(8,128)} copy(f32[32,64]{1,0:T(8,128)S(1)} %shard_map.37) | data formatting | bytes 16384
Async XLA Ops:
  0.0 0.9 %copy-start = (s32[1024,32]{0,1:T(8,128)S(1)}, s32[1024,32]{0,1:T(8,128)}, u32[]{:S(2)}) copy-start(s32[1024,32]{0,1:T(8,128)} %param.4) | copy-start | bytes 393220
  0.9 0.7 %copy-start.1 = (s32[1024]{0:T(1024)S(1)}, s32[1024]{0:T(1024)}, u32[]{:S(2)}) copy-start(s32[1024]{0:T(1024)} %param.5) | copy-start | bytes 12292

commit v2 on v1

--- a/solution.py
+++ b/solution.py
@@ -82,7 +82,6 @@
 
     allele_copy = pltpu.make_async_copy(allele_hbm, allele, small_sem.at[0])
     owner_copy = pltpu.make_async_copy(owner_hbm, owner, small_sem.at[1])
-    owner_copy.start()
     allele_copy.start()
     post_copies = []
     for i in range(steps):
@@ -90,6 +89,8 @@
         copy = pltpu.make_async_copy(post_hbm.at[:, rows, :], post.at[:, rows, :], post_sem.at[i])
         copy.start()
         post_copies.append(copy)
+        if i == 0:
+            owner_copy.start()
 
     barrier = pltpu.get_barrier_semaphore()
     for step in range(1, chips):
@@ -97,28 +98,7 @@
     for step in range(1, group):
         pl.semaphore_signal(barrier, inc=1, device_id=group_peer(step), device_id_type=MESH)
 
-    owner_copy.wait()
-    owners = owner[...]
-    table = (lax.broadcasted_iota(jnp.int32, (devices, targets), 0) == owners).astype(F32)
-    before = (
-        lax.broadcasted_iota(jnp.int32, (LANES, LANES), 0)
-        < lax.broadcasted_iota(jnp.int32, (LANES, LANES), 1)
-    ).astype(F32).astype(BF16)
-    carry = jnp.zeros((devices, 1), F32)
-    ranks = []
-    for b in range(targets // LANES):
-        piece = table[:, b * LANES : (b + 1) * LANES]
-        count = jnp.dot(piece.astype(BF16), before, preferred_element_type=F32) + carry
-        ranks.append(jnp.sum(piece * count, axis=0, keepdims=True))
-        carry = carry + jnp.sum(piece, axis=1, keepdims=True)
-    row_of = owners.astype(F32) * per_device + jnp.concatenate(ranks, axis=1)
-
     order = sorted(range(1, chips), key=lambda s: abs(s - chips // 2 - 0.5)) + [0]
-
-    for step in order:
-        first = ((chip + step) % chips) * per_chip
-        wanted = (lax.broadcasted_iota(jnp.int32, (per_chip, targets), 0) + first).astype(F32)
-        choose[step] = (wanted == row_of).astype(F32).astype(BF16)
 
     allele_copy.wait()
     col = lax.broadcasted_iota(jnp.int32, (block, LANES), 1)
@@ -152,6 +132,26 @@
     for i in range(steps):
         rows = pl.ds(i * chunk, chunk)
         post_copies[i].wait()
+        if i == 0:
+            owner_copy.wait()
+            owners = owner[...]
+            table = (lax.broadcasted_iota(jnp.int32, (devices, targets), 0) == owners).astype(F32)
+            before = (
+                lax.broadcasted_iota(jnp.int32, (LANES, LANES), 0)
+                < lax.broadcasted_iota(jnp.int32, (LANES, LANES), 1)
+            ).astype(F32).astype(BF16)
+            carry = jnp.zeros((devices, 1), F32)
+            ranks = []
+            for b in range(targets // LANES):
+                piece = table[:, b * LANES : (b + 1) * LANES]
+                count = jnp.dot(piece.astype(BF16), before, preferred_element_type=F32) + carry
+                ranks.append(jnp.sum(piece * count, axis=0, keepdims=True))
+                carry = carry + jnp.sum(piece, axis=1, keepdims=True)
+            row_of = owners.astype(F32) * per_device + jnp.concatenate(ranks, axis=1)
+        for step in order[i::steps]:
+            first = ((chip + step) % chips) * per_chip
+            wanted = (lax.broadcasted_iota(jnp.int32, (per_chip, targets), 0) + first).astype(F32)
+            choose[step] = (wanted == row_of).astype(F32).astype(BF16)
         total = jnp.dot(post[0, rows, :], weights[0], preferred_element_type=F32)
         for k in range(1, anchors):
             total = total + jnp.dot(post[k, rows, :], weights[k], preferred_element_type=F32)
@@ -164,7 +164,25 @@
     kept = pl.ds(pl.multiple_of(core * rows_kept, 8), rows_kept)
     given = pl.ds(pl.multiple_of((1 - core) * rows_kept, 8), rows_kept)
     pair_copies = {}
-    for step in order:
+    chip_copies = {}
+    lag = 3
+
+    def pass_on(step):
+        pair_copies[step].wait_recv()
+        reduced[step] = mine[step, kept, :] + pair_in[step]
+        if step:
+            copy = pltpu.make_async_remote_copy(
+                src_ref=reduced.at[step],
+                dst_ref=chip_in.at[step],
+                send_sem=chip_send.at[step],
+                recv_sem=chip_recv.at[step],
+                device_id=chip_peer(step),
+                device_id_type=MESH,
+            )
+            copy.start()
+            chip_copies[step] = copy
+
+    for at, step in enumerate(order):
         both = jnp.dot(choose[step], parts[...], preferred_element_type=F32)
         sums = jnp.transpose(both[:, :LANES] + both[:, LANES:])
         for c in range(CORES):
@@ -179,22 +197,11 @@
         )
         copy.start()
         pair_copies[step] = copy
-
-    chip_copies = {}
-    for step in order:
-        pair_copies[step].wait_recv()
-        reduced[step] = mine[step, kept, :] + pair_in[step]
-        if step:
-            copy = pltpu.make_async_remote_copy(
-                src_ref=reduced.at[step],
-                dst_ref=chip_in.at[step],
-                send_sem=chip_send.at[step],
-                recv_sem=chip_recv.at[step],
-                device_id=chip_peer(step),
-                device_id_type=MESH,
-            )
-            copy.start()
-            chip_copies[step] = copy
+        if at >= lag:
+            pass_on(order[at - lag])
+
+    for step in order[-lag:]:
+        pass_on(step)
 
     total = reduced[0]
     for step in reversed(order[:-1]):

time: 23.5 us -> 22.6 us (0.962)
  Pallas kernels: 21.1 us -> 20.3 us
    pallas_call x1, Pallas kernels: 21.1 us -> 20.3 us  [on_device(): pl.pallas_call(functools.partial(kernel, hap_count, mk_count, steps), out...]
where the time goes in v2:
time: 22.6 us; the launch traced here: 22.5 us
  Pallas kernels  20.3 us (90%)
  local copies, waits for them, and re-layouts  2.2 us (10%)
    pallas_call x1, Pallas kernels, on_device(): pl.pallas_call(functools.partial(kernel, hap_count, mk_count, steps), out...  20.3 us
    unnamed x5, local copies, waits for them, and re-layouts  2.2 us

profile of v2, /device:TPU:0, one launch (start us, length us, event | category | flops | bytes accessed | tf_op | source)
XLA Modules:
  0.0 22.5 jit_solution(6736243850752889847)
XLA Ops:
  0.0 0.0 copy-start
  0.0 0.9 %copy-done = s32[1024,32]{0,1:T(8,128)S(1)} copy-done((s32[1024,32]{0,1:T(8,128)S(1)}, s32[1024,32]{0,1:T(8,128)}, u32[]{:S(2)}) %copy-start) | copy-done | bytes 131096
  0.9 0.0 copy-start.1
  0.9 0.7 %copy-done.1 = s32[1024]{0:T(1024)S(1)} copy-done((s32[1024]{0:T(1024)S(1)}, s32[1024]{0:T(1024)}, u32[]{:S(2)}) %copy-start.1) | copy-done | bytes 4120
  1.6 20.3 %shard_map.37 = f32[32,64]{1,0:T(8,128)S(1)} custom-call(bf16[5,1024,1024]{2,1,0:T(8,128)(2,1)} %post_hbm.1, s32[32,1024]{1,0:T(8,128)S(1)} %bitcast.2, s32[1,1024]{1,0:T(1,128)S(1)} %bitcast.3), custom_call_target="tpu_custom_call" | custom-call | tf_op jit(solution)/shard_map/pallas_call | solution.py:284
  21.9 0.6 %copy.5 = f32[32,64]{1,0:T(8,128)} copy(f32[32,64]{1,0:T(8,128)S(1)} %shard_map.37) | data formatting | bytes 16384
Async XLA Ops:
  0.0 0.9 %copy-start = (s32[1024,32]{0,1:T(8,128)S(1)}, s32[1024,32]{0,1:T(8,128)}, u32[]{:S(2)}) copy-start(s32[1024,32]{0,1:T(8,128)} %param.4) | copy-start | bytes 393220
  0.9 0.7 %copy-start.1 = (s32[1024]{0:T(1024)S(1)}, s32[1024]{0:T(1024)}, u32[]{:S(2)}) copy-start(s32[1024]{0:T(1024)} %param.5) | copy-start | bytes 12292
